TPU v7x, 128 devices: a whole 4x4x4 slice. The times are simulated.
128 devices in a mesh: data: 1, sp: 128 (over z, y, x, core).
Axes of the slice: x: 4, y: 4, z: 4, core: 2. Of those that a mesh axis runs over, the one named last changes fastest.
Arguments:
- latents: bfloat16 [1, 256, 256, 384], P('data', 'sp')
- norms: float32 [4, 4, 384], replicated
- w_qkv: bfloat16 [4, 384, 3, 6, 64], replicated
- w_out: bfloat16 [4, 6, 64, 384], replicated
- w_up: bfloat16 [4, 384, 1536], replicated
- w_down: bfloat16 [4, 1536, 384], replicated
Outputs:
- output: bfloat16 [1, 256, 256, 384], P('data', None, 'sp')
All inputs are finite; a program needn't handle non-finite values.
Results may differ from a plain program's by a relative error of at most 0.015725.
Values are sent between devices in bfloat16 or wider.
A program may use at most 1 GiB of HBM per device.

v0:
```python
import math
import jax
import jax.numpy as jnp
from jax import lax
from jax.sharding import PartitionSpec as P

EPS = 1e-6
SPATIAL = (2, 'btqhe,btkhe->bthqk', 'bthqk,btkhe->btqhe')
TEMPORAL = (1, 'bqshe,bkshe->bshqk', 'bshqk,bkshe->bqshe')


def layer_norm(tokens, norm_gain, norm_shift):
    tokens_f32 = tokens.astype(jnp.float32)
    row_mean = jnp.mean(tokens_f32, axis=-1, keepdims=True)
    centered = tokens_f32 - row_mean
    variance = jnp.mean(jnp.square(centered), axis=-1, keepdims=True)
    return (centered * lax.rsqrt(variance + EPS) * norm_gain + norm_shift).astype(jnp.bfloat16)


def attention(query_rows, key_rows, value_rows, layout):
    seq_axis, score_form, mix_form = layout
    seq_len = query_rows.shape[seq_axis]
    q_block = math.gcd(seq_len, 128)
    logit_scale = query_rows.shape[-1] ** -0.5

    def attend_block(block_idx, attn_out):
        q_start = block_idx * q_block
        q_part = lax.dynamic_slice_in_dim(query_rows, q_start, q_block, axis=seq_axis)
        logits = jnp.einsum(score_form, q_part, key_rows, preferred_element_type=jnp.float32) * logit_scale
        attn_probs = jax.nn.softmax(logits, axis=-1).astype(jnp.bfloat16)
        block_out = jnp.einsum(mix_form, attn_probs, value_rows, preferred_element_type=jnp.float32).astype(jnp.bfloat16)
        return lax.dynamic_update_slice_in_dim(attn_out, block_out, q_start, axis=seq_axis)

    return lax.fori_loop(0, seq_len // q_block, attend_block, jnp.zeros_like(query_rows))


def project_heads(normed, head_weight):
    return jnp.einsum('btsd,dhe->btshe', normed, head_weight, preferred_element_type=jnp.float32).astype(jnp.bfloat16)


def transformer_block(tokens, norm_rows, qkv_weight, out_weight, up_weight, down_weight, layout):
    normed = layer_norm(tokens, norm_rows[0], norm_rows[1])
    mixed_heads = attention(project_heads(normed, qkv_weight[:, 0]), project_heads(normed, qkv_weight[:, 1]), project_heads(normed, qkv_weight[:, 2]), layout)
    attn_proj = jnp.einsum('btshe,hed->btsd', mixed_heads, out_weight, preferred_element_type=jnp.float32)
    residual = (tokens.astype(jnp.float32) + attn_proj).astype(jnp.bfloat16)
    normed_mlp = layer_norm(residual, norm_rows[2], norm_rows[3])
    up_proj = jnp.einsum('btsd,df->btsf', normed_mlp, up_weight, preferred_element_type=jnp.float32)
    hidden = jax.nn.gelu(up_proj, approximate=True).astype(jnp.bfloat16)
    down_proj = jnp.einsum('btsf,fd->btsd', hidden, down_weight, preferred_element_type=jnp.float32)
    return (residual.astype(jnp.float32) + down_proj).astype(jnp.bfloat16)


def solution(mesh):
    def local_stack(latents, norms, w_qkv, w_out, w_up, w_down):
        tokens = latents
        for layer_idx in range(w_qkv.shape[0]):
            if layer_idx % 2 == 1:
                tokens = lax.all_to_all(tokens, 'sp', 2, 1, tiled=True)
                layout = TEMPORAL
            else:
                if layer_idx > 0:
                    tokens = lax.all_to_all(tokens, 'sp', 1, 2, tiled=True)
                layout = SPATIAL
            tokens = transformer_block(tokens, norms[layer_idx], w_qkv[layer_idx], w_out[layer_idx], w_up[layer_idx], w_down[layer_idx], layout)
        return tokens

    replicated = P()
    return jax.shard_map(local_stack, mesh=mesh, in_specs=(P('data', 'sp', None, None), replicated, replicated, replicated, replicated, replicated), out_specs=P('data', None, 'sp', None), check_vma=False)
```

profile of v0, /device:TPU:1, one launch (start us, length us, event | category | flops | bytes accessed | tf_op | source)
XLA Modules:
  0.0 137.6 jit_solution(1273771184454265301)
XLA Ops:
  1.0 3.7 %slice_bitcast_fusion = (bf16[384,3,6,64]{0,3,2,1:T(8,128)(2,1)S(1)}, bf16[384,3,6,64]{0,3,2,1:T(8,128)(2,1)}, bf16[384,3,6,64]{0,3,2,1:T(8,128)(2,1)S(1)}, bf16[384,3,6,64]{0,3,2,1:T(8,128)(2,1)}) fusion(bf16[4,384,3,6,64]{1,4,3,2,0:T(8,128)(2,1)} %param.16), kind=kLoop, calls=%fused_computation.172 | loop fusion | bytes 7077888 | tf_op jit(solution)/shard_map/squeeze | solution.py:64
  8.4 6.0 %while.52 = (s32[]{:T(128)}, bf16[1,2,256,6,64]{2,4,3,1,0:T(8,128)(2,1)}, bf16[1,2,256,6,64]{2,4,3,1,0:T(8,128)(2,1)S(1)}, bf16[1,2,256,6,64]{2,4,3,1,0:T(8,128)...) while((s32[]{:T(128)}, ...), condition=%wide.region_5.0_spmd, body=%wide.region_2.0_spmd.sunk | while | flops 102727936 | bytes 4337811 | solution.py:34
  9.2 2.1 %fusion.321 = bf16[1,2,256,6,64]{2,4,3,1,0:T(8,128)(2,1)} fusion(bf16[1,2,256,6,64]{2,4,3,1,0:T(8,128)(2,1)} %get-tuple-element.611, s32[]{:T(128)S(6)} %select_n.36, f32[2,6,128,256]{3,2,1,0:T(8,128)S(1)} %get-tuple-element.578, f32[2,6,128]{2,1,0:T(8,128)S(1)} %get-tuple-element.579, bf16[1,2,256,6,64]{2,4,3,1,0:T(8,128)(2,1)} %get-tuple-element.623), kind=kOutput, calls=%fused_computation.7.clone.1 | convolution fusion | flops 51216384 | bytes 2168836 | tf_op jit(solution)/shard_map/while/body/eval_jaxpr/bthqk,btkhe->btqhe/dot_general | solution.py:31
  12.2 2.2 %fusion.321 = bf16[1,2,256,6,64]{2,4,3,1,0:T(8,128)(2,1)} fusion(bf16[1,2,256,6,64]{2,4,3,1,0:T(8,128)(2,1)} %get-tuple-element.611, s32[]{:T(128)S(6)} %select_n.36, f32[2,6,128,256]{3,2,1,0:T(8,128)S(1)} %get-tuple-element.578, f32[2,6,128]{2,1,0:T(8,128)S(1)} %get-tuple-element.579, bf16[1,2,256,6,64]{2,4,3,1,0:T(8,128)(2,1)} %get-tuple-element.623), kind=kOutput, calls=%fused_computation.7.clone.1 | convolution fusion | flops 51216384 | bytes 2168836 | tf_op jit(solution)/shard_map/while/body/eval_jaxpr/bthqk,btkhe->btqhe/dot_general | solution.py:31
  14.4 1.7 %fusion.281 = (f32[2,256]{1,0:T(2,128)S(1)}, f32[1,2,256,384]{3,2,1,0:T(8,128)S(1)}) fusion(bf16[4,6,64,384]{3,2,1,0:T(8,128)(2,1)} %param.17, bf16[1,2,256,6,64]{2,4,3,1,0:T(8,128)(2,1)} %get-tuple-element.381, bf16[1,2,256,384]{3,2,1,0:T(8,128)(2,1)} %param.14), kind=kOutput, calls=%fused_computation.303 | convolution fusion | flops 151977472 | bytes 1869824 | tf_op jit(solution)/shard_map/btshe,hed->btsd/dot_general | solution.py:44
  16.4 3.6 %fusion.131 = bf16[1,2,256,384]{3,2,1,0:T(8,128)(2,1)S(1)} fusion(f32[1,2,256,384]{3,2,1,0:T(8,128)S(1)} %get-tuple-element.454, bf16[4,1536,384]{2,1,0:T(8,128)(2,1)} %param.19, bf16[4,384,1536]{2,1,0:T(8,128)(2,1)} %param.18, f32[384]{0:T(512)S(1)} %get-tuple-element.396, f32[384]{0:T(512)S(1)} %get-tuple-element.397, f32[2,256]{1,0:T(2,128)S(1)} %add_rsqrt_fusion.6, ...), kind=kOutput, calls=%fused_computation.119 | convolution fusion | flops 1216413696 | bytes 4333568 | tf_op jit(solution)/shard_map/btsf,fd->btsd/dot_general | solution.py:49
  21.1 11.5 %all-to-all-start = ((bf16[1,2,256,384]{3,1,0,2:T(2,128)(2,1)}), bf16[1,2,256,384]{3,1,0,2:T(2,128)(2,1)S(1)}, u32[]{:S(2)}, u32[]{:S(2)}) async-start(bf16[1,2,256,384]{3,1,0,2:T(2,128)(2,1)} %copy.14), calls=%async_computation | async-start | bytes 786432 | tf_op jit(solution)/shard_map/all_to_all | solution.py:58
  32.6 12.0 %all-to-all-done = bf16[1,2,256,384]{3,1,0,2:T(2,128)(2,1)S(1)} async-done(((bf16[1,2,256,384]{3,1,0,2:T(2,128)(2,1)}), bf16[1,2,256,384]{3,1,0,2:T(2,128)(2,1)S(1)}, u32[]{:S(2)}, u32[]{:S(2)}) %all-to-all-start) | async-done | bytes 393248 | tf_op jit(solution)/shard_map/all_to_all | solution.py:58
  50.8 6.0 %while.53 = (s32[]{:T(128)}, bf16[1,256,2,6,64]{1,4,3,2,0:T(8,128)(2,1)}, bf16[1,256,2,6,64]{1,4,3,2,0:T(8,128)(2,1)S(1)}, bf16[1,256,2,6,64]{1,4,3,2,0:T(8,128)...) while((s32[]{:T(128)}, ...), condition=%wide.region_13.0_spmd, body=%wide.region_10.0_spmd.sunk | while | flops 102727936 | bytes 4337811 | solution.py:34
  51.7 2.2 %fusion.326 = bf16[1,256,2,6,64]{1,4,3,2,0:T(8,128)(2,1)} fusion(bf16[1,256,2,6,64]{1,4,3,2,0:T(8,128)(2,1)} %get-tuple-element.638, s32[]{:T(128)S(6)} %select_n.37, f32[2,6,128,256]{3,2,1,0:T(8,128)S(1)} %get-tuple-element.585, f32[2,6,128]{2,1,0:T(8,128)S(1)} %get-tuple-element.586, bf16[1,256,2,6,64]{1,4,3,2,0:T(8,128)(2,1)} %get-tuple-element.650), kind=kOutput, calls=%fused_computation.23.clone.1 | convolution fusion | flops 51216384 | bytes 2168836 | tf_op jit(solution)/shard_map/while/body/eval_jaxpr/bshqk,bkshe->bqshe/dot_general | solution.py:31
  54.7 2.2 %fusion.326 = bf16[1,256,2,6,64]{1,4,3,2,0:T(8,128)(2,1)} fusion(bf16[1,256,2,6,64]{1,4,3,2,0:T(8,128)(2,1)} %get-tuple-element.638, s32[]{:T(128)S(6)} %select_n.37, f32[2,6,128,256]{3,2,1,0:T(8,128)S(1)} %get-tuple-element.585, f32[2,6,128]{2,1,0:T(8,128)S(1)} %get-tuple-element.586, bf16[1,256,2,6,64]{1,4,3,2,0:T(8,128)(2,1)} %get-tuple-element.650), kind=kOutput, calls=%fused_computation.23.clone.1 | convolution fusion | flops 51216384 | bytes 2168836 | tf_op jit(solution)/shard_map/while/body/eval_jaxpr/bshqk,bkshe->bqshe/dot_general | solution.py:31
  60.3 3.6 %fusion.151 = bf16[1,256,2,384]{3,1,2,0:T(8,128)(2,1)S(1)} fusion(f32[256,2,384]{2,0,1:T(8,128)S(1)} %get-tuple-element.456, bf16[4,1536,384]{2,1,0:T(8,128)(2,1)} %param.19, bf16[4,384,1536]{2,1,0:T(8,128)(2,1)} %param.18, f32[384]{0:T(512)S(1)} %get-tuple-element.392, f32[384]{0:T(512)S(1)} %get-tuple-element.393, f32[256,2]{0,1:T(2,128)S(1)} %add_rsqrt_fusion.5, ...), kind=kOutput, calls=%fused_computation.151 | convolution fusion | flops 1216413696 | bytes 4333568 | tf_op jit(solution)/shard_map/btsf,fd->btsd/dot_general | solution.py:49
  65.1 4.7 %all-to-all-start.1 = ((bf16[1,256,2,384]{3,2,0,1:T(2,128)(2,1)}), bf16[1,256,2,384]{3,2,0,1:T(2,128)(2,1)S(1)}, u32[]{:S(2)}, u32[]{:S(2)}) async-start(bf16[1,256,2,384]{3,2,0,1:T(2,128)(2,1)} %copy.16), calls=%async_computation.1 | async-start | bytes 786432 | tf_op jit(solution)/shard_map/all_to_all | solution.py:62
  69.7 12.0 %all-to-all-done.1 = bf16[1,256,2,384]{3,2,0,1:T(2,128)(2,1)S(1)} async-done(((bf16[1,256,2,384]{3,2,0,1:T(2,128)(2,1)}), bf16[1,256,2,384]{3,2,0,1:T(2,128)(2,1)S(1)}, u32[]{:S(2)}, u32[]{:S(2)}) %all-to-all-start.1) | async-done | bytes 393248 | tf_op jit(solution)/shard_map/all_to_all | solution.py:62
  87.9 6.0 %while.54 = (s32[]{:T(128)}, bf16[1,2,256,6,64]{2,4,3,1,0:T(8,128)(2,1)}, bf16[1,2,256,6,64]{2,4,3,1,0:T(8,128)(2,1)S(1)}, bf16[1,2,256,6,64]{2,4,3,1,0:T(8,128)...) while((s32[]{:T(128)}, ...), condition=%wide.region_21.0_spmd, body=%wide.region_18.0_spmd.sunk | while | flops 102727936 | bytes 4337811 | solution.py:34
  88.7 2.2 %fusion.331 = bf16[1,2,256,6,64]{2,4,3,1,0:T(8,128)(2,1)} fusion(bf16[1,2,256,6,64]{2,4,3,1,0:T(8,128)(2,1)} %get-tuple-element.665, s32[]{:T(128)S(6)} %select_n.38, f32[2,6,128,256]{3,2,1,0:T(8,128)S(1)} %get-tuple-element.592, f32[2,6,128]{2,1,0:T(8,128)S(1)} %get-tuple-element.593, bf16[1,2,256,6,64]{2,4,3,1,0:T(8,128)(2,1)} %get-tuple-element.677), kind=kOutput, calls=%fused_computation.39.clone.1 | convolution fusion | flops 51216384 | bytes 2168836 | tf_op jit(solution)/shard_map/while/body/eval_jaxpr/bthqk,btkhe->btqhe/dot_general | solution.py:31
  91.7 2.2 %fusion.331 = bf16[1,2,256,6,64]{2,4,3,1,0:T(8,128)(2,1)} fusion(bf16[1,2,256,6,64]{2,4,3,1,0:T(8,128)(2,1)} %get-tuple-element.665, s32[]{:T(128)S(6)} %select_n.38, f32[2,6,128,256]{3,2,1,0:T(8,128)S(1)} %get-tuple-element.592, f32[2,6,128]{2,1,0:T(8,128)S(1)} %get-tuple-element.593, bf16[1,2,256,6,64]{2,4,3,1,0:T(8,128)(2,1)} %get-tuple-element.677), kind=kOutput, calls=%fused_computation.39.clone.1 | convolution fusion | flops 51216384 | bytes 2168836 | tf_op jit(solution)/shard_map/while/body/eval_jaxpr/bthqk,btkhe->btqhe/dot_general | solution.py:31
  97.4 3.6 %fusion.150 = bf16[1,2,256,384]{3,2,1,0:T(8,128)(2,1)S(1)} fusion(f32[2,256,384]{2,1,0:T(8,128)S(1)} %get-tuple-element.458, bf16[4,1536,384]{2,1,0:T(8,128)(2,1)} %param.19, bf16[4,384,1536]{2,1,0:T(8,128)(2,1)} %param.18, f32[384]{0:T(512)S(1)} %get-tuple-element.388, f32[384]{0:T(512)S(1)} %get-tuple-element.389, f32[2,256]{1,0:T(2,128)S(1)} %add_rsqrt_fusion.4, ...), kind=kOutput, calls=%fused_computation.150 | convolution fusion | flops 1216413696 | bytes 4333568 | tf_op jit(solution)/shard_map/btsf,fd->btsd/dot_general | solution.py:49
  102.2 4.7 %all-to-all-start.2 = ((bf16[1,2,256,384]{3,1,0,2:T(2,128)(2,1)}), bf16[1,2,256,384]{3,1,0,2:T(2,128)(2,1)S(1)}, u32[]{:S(2)}, u32[]{:S(2)}) async-start(bf16[1,2,256,384]{3,1,0,2:T(2,128)(2,1)} %copy.18), calls=%async_computation.2 | async-start | bytes 786432 | tf_op jit(solution)/shard_map/all_to_all | solution.py:58
  106.8 12.0 %all-to-all-done.2 = bf16[1,2,256,384]{3,1,0,2:T(2,128)(2,1)S(1)} async-done(((bf16[1,2,256,384]{3,1,0,2:T(2,128)(2,1)}), bf16[1,2,256,384]{3,1,0,2:T(2,128)(2,1)S(1)}, u32[]{:S(2)}, u32[]{:S(2)}) %all-to-all-start.2) | async-done | bytes 393248 | tf_op jit(solution)/shard_map/all_to_all | solution.py:58
  124.1 6.0 %while.55 = (s32[]{:T(128)}, bf16[1,256,2,6,64]{1,4,3,2,0:T(8,128)(2,1)}, bf16[1,256,2,6,64]{1,4,3,2,0:T(8,128)(2,1)S(1)}, bf16[1,256,2,6,64]{1,4,3,2,0:T(8,128)...) while((s32[]{:T(128)}, ...), condition=%wide.region_29.0_spmd, body=%wide.region_26.0_spmd.sunk | while | flops 102727936 | bytes 4337811 | solution.py:34
  124.9 2.2 %fusion.336 = bf16[1,256,2,6,64]{1,4,3,2,0:T(8,128)(2,1)} fusion(bf16[1,256,2,6,64]{1,4,3,2,0:T(8,128)(2,1)} %get-tuple-element.692, s32[]{:T(128)S(6)} %select_n.39, f32[2,6,128,256]{3,2,1,0:T(8,128)S(1)} %get-tuple-element.599, f32[2,6,128]{2,1,0:T(8,128)S(1)} %get-tuple-element.600, bf16[1,256,2,6,64]{1,4,3,2,0:T(8,128)(2,1)} %get-tuple-element.704), kind=kOutput, calls=%fused_computation.55.clone.1 | convolution fusion | flops 51216384 | bytes 2168836 | tf_op jit(solution)/shard_map/while/body/eval_jaxpr/bshqk,bkshe->bqshe/dot_general | solution.py:31
  127.9 2.1 %fusion.336 = bf16[1,256,2,6,64]{1,4,3,2,0:T(8,128)(2,1)} fusion(bf16[1,256,2,6,64]{1,4,3,2,0:T(8,128)(2,1)} %get-tuple-element.692, s32[]{:T(128)S(6)} %select_n.39, f32[2,6,128,256]{3,2,1,0:T(8,128)S(1)} %get-tuple-element.599, f32[2,6,128]{2,1,0:T(8,128)S(1)} %get-tuple-element.600, bf16[1,256,2,6,64]{1,4,3,2,0:T(8,128)(2,1)} %get-tuple-element.704), kind=kOutput, calls=%fused_computation.55.clone.1 | convolution fusion | flops 51216384 | bytes 2168836 | tf_op jit(solution)/shard_map/while/body/eval_jaxpr/bshqk,bkshe->bqshe/dot_general | solution.py:31
  132.9 3.6 %fusion.149 = bf16[1,256,2,384]{3,1,2,0:T(8,128)(2,1)S(1)} fusion(f32[256,2,384]{2,0,1:T(8,128)S(1)} %get-tuple-element.460, bf16[4,1536,384]{2,1,0:T(8,128)(2,1)} %param.19, bf16[4,384,1536]{2,1,0:T(8,128)(2,1)} %param.18, f32[384]{0:T(512)S(1)} %get-tuple-element.400, f32[384]{0:T(512)S(1)} %get-tuple-element.385, f32[256,2]{0,1:T(2,128)S(1)} %add_rsqrt_fusion.3, ...), kind=kOutput, calls=%fused_computation.149 | convolution fusion | flops 1216413696 | bytes 4333568 | tf_op jit(solution)/shard_map/btsf,fd->btsd/dot_general | solution.py:49
  (84 shorter events, 43.4 us)
Async XLA Ops:
  1.0 3.7 %copy-start.2 = (bf16[1,2,256,384]{3,2,1,0:T(8,128)(2,1)S(1)}, bf16[1,2,256,384]{3,2,1,0:T(8,128)(2,1)}, u32[]{:S(2)}) copy-start(bf16[1,2,256,384]{3,2,1,0:T(8,128)(2,1)} %param.14) | copy-start | bytes 1179652
  21.1 23.5 %all-to-all-start = ((bf16[1,2,256,384]{3,1,0,2:T(2,128)(2,1)}), bf16[1,2,256,384]{3,1,0,2:T(2,128)(2,1)S(1)}, u32[]{:S(2)}, u32[]{:S(2)}) async-start(bf16[1,2,256,384]{3,1,0,2:T(2,128)(2,1)} %copy.14), calls=%async_computation | async-start | bytes 786432 | tf_op jit(solution)/shard_map/all_to_all | solution.py:58
  45.0 1.9 %copy-start.1 = (bf16[384,3,6,64]{0,3,2,1:T(8,128)(2,1)S(1)}, bf16[384,3,6,64]{0,3,2,1:T(8,128)(2,1)}, u32[]{:S(2)}) copy-start(bf16[384,3,6,64]{0,3,2,1:T(8,128)(2,1)} %get-tuple-element.450) | copy-start | bytes 2654212
  56.8 1.7 %copy-start.4 = (bf16[1,256,2,6,64]{1,4,3,2,0:T(8,128)(2,1)S(1)}, bf16[1,256,2,6,64]{1,4,3,2,0:T(8,128)(2,1)}, u32[]{:S(2)}) copy-start(bf16[1,256,2,6,64]{1,4,3,2,0:T(8,128)(2,1)} %get-tuple-element.382) | copy-start | bytes 1179652
  65.1 16.7 %all-to-all-start.1 = ((bf16[1,256,2,384]{3,2,0,1:T(2,128)(2,1)}), bf16[1,256,2,384]{3,2,0,1:T(2,128)(2,1)S(1)}, u32[]{:S(2)}, u32[]{:S(2)}) async-start(bf16[1,256,2,384]{3,2,0,1:T(2,128)(2,1)} %copy.16), calls=%async_computation.1 | async-start | bytes 786432 | tf_op jit(solution)/shard_map/all_to_all | solution.py:62
  82.1 1.9 %copy-start = (bf16[384,3,6,64]{0,3,2,1:T(8,128)(2,1)S(1)}, bf16[384,3,6,64]{0,3,2,1:T(8,128)(2,1)}, u32[]{:S(2)}) copy-start(bf16[384,3,6,64]{0,3,2,1:T(8,128)(2,1)} %get-tuple-element.452) | copy-start | bytes 2654212
  93.9 1.7 %copy-start.5 = (bf16[1,2,256,6,64]{2,4,3,1,0:T(8,128)(2,1)S(1)}, bf16[1,2,256,6,64]{2,4,3,1,0:T(8,128)(2,1)}, u32[]{:S(2)}) copy-start(bf16[1,2,256,6,64]{2,4,3,1,0:T(8,128)(2,1)} %get-tuple-element.383) | copy-start | bytes 1179652
  102.2 16.7 %all-to-all-start.2 = ((bf16[1,2,256,384]{3,1,0,2:T(2,128)(2,1)}), bf16[1,2,256,384]{3,1,0,2:T(2,128)(2,1)S(1)}, u32[]{:S(2)}, u32[]{:S(2)}) async-start(bf16[1,2,256,384]{3,1,0,2:T(2,128)(2,1)} %copy.18), calls=%async_computation.2 | async-start | bytes 786432 | tf_op jit(solution)/shard_map/all_to_all | solution.py:58
  130.1 1.0 copy-start.3
where the time goes:
time: 139 us; the launch traced here: 138 us
  matrix products  52.8 us (38%)
  waiting for transfers between devices  36 us (26%)
  starting transfers between devices  20.8 us (15%)
  local copies, waits for them, and re-layouts  17.3 us (12%)
  other arithmetic  10.3 us (7%)
    all_to_all x2, waiting for transfers between devices, local_stack(): tokens = lax.all_to_all(tokens, 'sp', 2, 1, tiled=True)  24 us
    dot_general x8, matrix products, attend_block(): jnp.einsum(mix_form, attn_probs, value_rows, preferred_element_type=jnp.f...  17.2 us
    all_to_all x2, starting transfers between devices, local_stack(): tokens = lax.all_to_all(tokens, 'sp', 2, 1, tiled=True)  16.2 us
    dot_general x4, matrix products, transformer_block(): jnp.einsum('btsf,fd->btsd', hidden, down_weight, preferred_element_type=j...  14.3 us
    all_to_all x1, waiting for transfers between devices, local_stack(): tokens = lax.all_to_all(tokens, 'sp', 1, 2, tiled=True)  12 us
    dot_general x12, matrix products, project_heads(): jnp.einsum('btsd,dhe->btshe', normed, head_weight, preferred_element_type...  8.21 us
    sub x8, matrix products, attend_block(): attn_probs = jax.nn.softmax(logits, axis=-1).astype(jnp.bfloat16)  6.82 us
    dot_general x4, matrix products, transformer_block(): jnp.einsum('btshe,hed->btsd', mixed_heads, out_weight, preferred_element_...  6.23 us
  transfers between devices with their start and end apart: 3, of which 3 were waited for; matrix products, arithmetic and copies ran while one was open for 0% of the time, Pallas kernels for 0%

commit v1 on v0

v1 whole, which is shorter than its diff:
```python
import functools
import math

import jax
import jax.numpy as jnp
from jax import lax
from jax.experimental import pallas as pl
from jax.experimental.pallas import tpu as pltpu
from jax.sharding import PartitionSpec as P

EPS = 1e-6
D = 384
QKV = 3 * D
HID = 4 * D
DEV = 128
BLOCKS = 4
CHUNKS = 2
SLOTS = DEV // CHUNKS
ROWS = 4 * SLOTS
HALF = ROWS // 2
EXP_SCALE = 64 ** -0.5 * math.log2(math.e)
GELU_A = math.sqrt(2.0 / math.pi)
GELU_B = GELU_A * 0.044715
BF = jnp.bfloat16
F32 = jnp.float32


def slot_table():
    hops = (0, 1, 2, 1)
    offs = [(z, y, x, c) for z in range(4) for y in range(4) for x in range(4) for c in range(2)]
    offs.sort(key=lambda o: (-(hops[o[0]] + hops[o[1]] + hops[o[2]]), -o[3], o))
    index = {o: k for k, o in enumerate(offs)}
    back = [index[((-o[0]) % 4, (-o[1]) % 4, (-o[2]) % 4, o[3])] for o in offs]
    return offs, back


OFFS, BACK = slot_table()


def layer_norm(u, gain, shift):
    mean = jnp.mean(u, axis=-1, keepdims=True)
    cen = u - mean
    var = jnp.mean(cen * cen, axis=-1, keepdims=True)
    return (cen * lax.rsqrt(var + EPS) * gain + shift).astype(BF)


def gelu(x):
    half = 0.5 * x
    return half + half * jnp.tanh(x * (GELU_A + GELU_B * (x * x)))


def put(ref, start, rows):
    for t in range(3):
        ref[t, pl.ds(start, SLOTS, stride=4), :] = rows[:, t * 128:(t + 1) * 128]


def take(ref, start):
    return jnp.concatenate([ref[t, pl.ds(start, SLOTS, stride=4), :] for t in range(3)], axis=1)


def dot(a, b):
    return jnp.dot(a, b, preferred_element_type=F32)


def stack_kernel(x_ref, tab_ref, norms_ref, wqkv_ref, wout_ref, wup_ref, wdown_ref, y_ref,
                 xv, wqkv, wout, wup, wdown, f_in, f_out, qkv_s, o_s, hid_s, zsend, recv,
                 x_sem, w_sem, send_sem, recv_sem, y_sem):
    me = lax.axis_index('sp')
    digits = (me // 32, (me // 8) % 4, (me // 2) % 4, me % 2)

    barrier = pltpu.get_barrier_semaphore()

    def greet(i, carry):
        pl.semaphore_signal(barrier, inc=1, device_id={'sp': lax.rem(me + i, DEV)}, device_id_type=pl.DeviceIdType.MESH)
        return carry

    x_copy = pltpu.make_async_copy(x_ref, xv, x_sem)
    x_copy.start()
    w_copies = []
    for l in range(BLOCKS):
        row = []
        for i, (src, dst) in enumerate(((wqkv_ref, wqkv), (wout_ref, wout), (wup_ref, wup), (wdown_ref, wdown))):
            cp = pltpu.make_async_copy(src.at[l], dst.at[l], w_sem.at[l, i])
            cp.start()
            row.append(cp)
        w_copies.append(row)
    lax.fori_loop(1, DEV, greet, 0)

    zpos = [(((digits[0] - d) + 4) % 4) * 32 for d in range(4)]
    ypos = [(((digits[1] - d) + 4) % 4) * 8 for d in range(4)]
    xpos = [(((digits[2] - d) + 4) % 4) * 2 for d in range(4)]
    cpos = [(digits[3] + d) % 2 for d in range(2)]

    def dev_of(k):
        o = OFFS[k]
        return zpos[o[0]] + ypos[o[1]] + xpos[o[2]] + cpos[o[3]]

    x_copy.wait()
    lane = lax.broadcasted_iota(jnp.int32, (HALF, 2 * DEV), 1)
    for c in range(CHUNKS):
        tab = tab_ref[c]
        dz = (digits[0] - tab[:, 0:1] + 4) % 4
        dy = (digits[1] - tab[:, 1:2] + 4) % 4
        dx = (digits[2] - tab[:, 2:3] + 4) % 4
        dc = (digits[3] + tab[:, 3:4]) % 2
        patch = 2 * (dz * 32 + dy * 8 + dx * 2 + dc) + tab[:, 4:5]
        pick = jnp.where(lane == patch, 1.0, 0.0).astype(BF)
        for a in range(2):
            rows = dot(pick, xv[a])
            for b in range(2):
                put(f_in, c * ROWS + 2 * a + b, rows[b * SLOTS:(b + 1) * SLOTS])

    low = lax.broadcasted_iota(jnp.int32, (HALF, 128), 1) < 64

    def load_rows(c):
        return jnp.concatenate([take(f_in, c * ROWS + 2 * j + i) for j in range(2) for i in range(2)], axis=0)

    for l in range(BLOCKS):
        gains = norms_ref[l]
        for c in range(CHUNKS):
            if l > 0:
                n = SLOTS - (c == CHUNKS - 1)
                got = recv.at[l - 1, pl.ds(c * SLOTS, n)]
                pltpu.make_async_copy(got, got, recv_sem.at[l - 1, c]).wait()
                if c == CHUNKS - 1:
                    recv[l - 1, DEV - 1] = zsend[l - 1, DEV - 1]
                rows = recv[l - 1, c * SLOTS:(c + 1) * SLOTS].reshape(ROWS, D).astype(F32)
                for t in range(3):
                    f_in[t, c * ROWS:(c + 1) * ROWS, :] = rows[:, t * 128:(t + 1) * 128]
            if c == 0:
                w_copies[l][0].wait()
            normed = layer_norm(load_rows(c), gains[0:1], gains[1:2])
            proj = dot(normed, wqkv[l]).astype(BF)
            for j in range(2):
                qkv_s[j, c * HALF:(c + 1) * HALF, :] = proj[j * HALF:(j + 1) * HALF]
        for c in range(CHUNKS):
            for j in range(2):
                for t in range(3):
                    q = qkv_s[j, c * HALF:(c + 1) * HALF, t * 128:(t + 1) * 128]
                    k = qkv_s[j, :, D + t * 128:D + (t + 1) * 128]
                    v = qkv_s[j, :, 2 * D + t * 128:2 * D + (t + 1) * 128]
                    zero = jnp.zeros_like(q)
                    qq = jnp.concatenate([jnp.where(low, q, zero), jnp.where(low, zero, q)], axis=0)
                    s = lax.dot_general(qq, k, (((1,), (1,)), ((), ())), preferred_element_type=F32)
                    e = jnp.exp2((s - jnp.max(s, axis=-1, keepdims=True)) * EXP_SCALE)
                    p = (e * (1.0 / jnp.sum(e, axis=-1, keepdims=True))).astype(BF)
                    oo = dot(p, v)
                    o_s[j * HALF:(j + 1) * HALF, t * 128:(t + 1) * 128] = jnp.where(low, oo[:HALF], oo[HALF:]).astype(BF)
            if c == 0:
                for cp in w_copies[l][1:]:
                    cp.wait()
            h = (load_rows(c) + dot(o_s[...], wout[l])).astype(BF).astype(F32)
            normed = layer_norm(h, gains[2:3], gains[3:4])
            for n in range(0, HID, 512):
                hid_s[:, n:n + 512] = gelu(dot(normed, wup[l, :, n:n + 512])).astype(BF)
            z = h + dot(hid_s[...], wdown[l])
            for j in range(2):
                for b in range(2):
                    put(f_out, 2 * b + j, z[(2 * j + b) * SLOTS:(2 * j + b + 1) * SLOTS])
            zs = jnp.concatenate([f_out[t] for t in range(3)], axis=1)
            zsend[l, c * SLOTS:(c + 1) * SLOTS] = zs.astype(BF).reshape(SLOTS, 4, D)
            if l == 0 and c == 0:
                pl.semaphore_wait(barrier, DEV - 1)
            for k in range(c * SLOTS, (c + 1) * SLOTS):
                if l == BLOCKS - 1:
                    pltpu.make_async_copy(zsend.at[l, k], y_ref.at[dev_of(k)], y_sem).start()
                elif k < DEV - 1:
                    pltpu.make_async_remote_copy(zsend.at[l, k], recv.at[l, BACK[k]], send_sem.at[l, c], recv_sem.at[l, c],
                                                 device_id={'sp': dev_of(k)}, device_id_type=pl.DeviceIdType.MESH).start()

    for l in range(BLOCKS - 1):
        for c in range(CHUNKS):
            n = SLOTS - (c == CHUNKS - 1)
            sent = zsend.at[l, pl.ds(c * SLOTS, n)]
            pltpu.make_async_copy(sent, sent, send_sem.at[l, c]).wait()
    pltpu.make_async_copy(zsend.at[BLOCKS - 1], y_ref, y_sem).wait()


def solution(mesh):
    table = [[list(OFFS[c * SLOTS + r % SLOTS]) + [r // SLOTS] for r in range(HALF)] for c in range(CHUNKS)]

    def local_stack(latents, norms, w_qkv, w_out, w_up, w_down):
        anywhere = pl.BlockSpec(memory_space=pl.ANY)
        vmem = pl.BlockSpec(memory_space=pltpu.VMEM)
        out = pl.pallas_call(
            stack_kernel,
            out_shape=jax.ShapeDtypeStruct((DEV, 4, D), BF),
            in_specs=[anywhere, vmem, vmem, anywhere, anywhere, anywhere, anywhere],
            out_specs=anywhere,
            scratch_shapes=[
                pltpu.VMEM((2, 2 * DEV, D), BF),
                pltpu.VMEM((BLOCKS, D, QKV), BF),
                pltpu.VMEM((BLOCKS, D, D), BF),
                pltpu.VMEM((BLOCKS, D, HID), BF),
                pltpu.VMEM((BLOCKS, HID, D), BF),
                pltpu.VMEM((3, 4 * DEV, 128), F32),
                pltpu.VMEM((3, ROWS, 128), F32),
                pltpu.VMEM((2, 2 * DEV, QKV), BF),
                pltpu.VMEM((ROWS, D), BF),
                pltpu.VMEM((ROWS, HID), BF),
                pltpu.VMEM((BLOCKS, DEV, 4, D), BF),
                pltpu.VMEM((BLOCKS - 1, DEV, 4, D), BF),
                pltpu.SemaphoreType.DMA,
                pltpu.SemaphoreType.DMA((BLOCKS, 4)),
                pltpu.SemaphoreType.DMA((BLOCKS - 1, CHUNKS)),
                pltpu.SemaphoreType.DMA((BLOCKS - 1, CHUNKS)),
                pltpu.SemaphoreType.DMA,
            ],
            compiler_params=pltpu.CompilerParams(collective_id=0, has_side_effects=True, vmem_limit_bytes=60 * 1024 * 1024),
            name='stack',
        )(latents.reshape(2, 2 * DEV, D), jnp.asarray(table, jnp.int32), norms, w_qkv.reshape(BLOCKS, D, QKV),
          w_out.reshape(BLOCKS, D, D), w_up, w_down)
        return out.reshape(1, 2 * DEV, 2, D)

    replicated = P()
    return jax.shard_map(local_stack, mesh=mesh, in_specs=(P('data', 'sp', None, None), replicated, replicated, replicated, replicated, replicated), out_specs=P('data', None, 'sp', None), check_vma=False)
```

time: 139 us -> 60.5 us (0.44)
  matrix products: 52.8 us -> 0 us
  Pallas kernels: 0 us -> 52.4 us
  waiting for transfers between devices: 36 us -> 0 us
  starting transfers between devices: 20.8 us -> 0 us
  other arithmetic: 10.3 us -> 0 us
  local copies, waits for them, and re-layouts: 17.3 us -> 7.69 us
    pallas_call x0 -> x1, Pallas kernels: none -> 52.4 us  [local_stack(): pl.pallas_call(stack_kernel, out_shape=jax.ShapeDtypeStruct((DEV, 4, D),...]
    dot_general x28 -> x0, matrix products: 46 us -> none  [the longest x8 17.2 us: attend_block(): jnp.einsum(mix_form, attn_probs, value_rows, preferred_element_type=jnp.f...]
    all_to_all x3 -> x0, waiting for transfers between devices: 36 us -> none  [the longest x2 24 us: local_stack(): tokens = lax.all_to_all(tokens, 'sp', 2, 1, tiled=True)]
    all_to_all x3 -> x0, starting transfers between devices: 20.8 us -> none  [the longest x2 16.2 us: local_stack(): tokens = lax.all_to_all(tokens, 'sp', 2, 1, tiled=True)]
    convert_element_type x10 -> x0, local copies, waits for them, and re-layouts: 9.04 us -> none  [the longest x4 4.6 us: transformer_block(): return (residual.astype(jnp.float32) + down_proj).astype(jnp.bfloat16)]
    reshape x0 -> x2, local copies, waits for them, and re-layouts: none -> 7.69 us  [the longest x1 5.77 us: local_stack(): w_qkv.reshape(BLOCKS, D, QKV)]
    sub x8 -> x0, matrix products: 6.82 us -> none  [attend_block(): attn_probs = jax.nn.softmax(logits, axis=-1).astype(jnp.bfloat16)]
    convert_element_type x6 -> x0, other arithmetic: 5.09 us -> none  [the longest x3 2.58 us: transformer_block(): residual = (tokens.astype(jnp.float32) + attn_proj).astype(jnp.bfloat16)]
  transfers between devices with their start and end apart: 3 -> 0, of which waited for: 3 -> 0; matrix products, arithmetic and copies ran while one was open for 0% -> 0% of each run, Pallas kernels for 0% -> 0%
where the time goes in v1:
time: 60.5 us; the launch traced here: 60.1 us
  Pallas kernels  52.4 us (87%)
  local copies, waits for them, and re-layouts  7.69 us (13%)
    pallas_call x1, Pallas kernels, local_stack(): pl.pallas_call(stack_kernel, out_shape=jax.ShapeDtypeStruct((DEV, 4, D),...  52.4 us
    reshape x1, local copies, waits for them, and re-layouts, local_stack(): w_qkv.reshape(BLOCKS, D, QKV)  5.77 us
    reshape x1, local copies, waits for them, and re-layouts, local_stack(): return out.reshape(1, 2 * DEV, 2, D)  1.92 us

profile of v1, /device:TPU:1, one launch (start us, length us, event | category | flops | bytes accessed | tf_op | source)
XLA Modules:
  0.0 60.1 jit_solution(8015017129405278696)
XLA Ops:
  0.0 5.8 %copy.9.wqkv_ref = bf16[4,384,1152]{2,1,0:T(8,128)(2,1)} copy(bf16[4,384,1152]{1,2,0:T(8,128)(2,1)} %bitcast.3) | data formatting | bytes 7077888 | tf_op jit(solution)/shard_map/reshape | solution.py:211
  5.8 52.4 %stack.1 = bf16[128,4,384]{2,1,0:T(4,128)(2,1)} custom-call(bf16[2,256,384]{2,1,0:T(8,128)(2,1)} %bitcast.5, s32[2,128,5]{2,1,0:T(8,128)} %constant.2.clone.tab_ref, f32[4,4,384]{2,1,0:T(4,128)} %norms_ref.1, bf16[4,384,1152]{2,1,0:T(8,128)(2,1)} %copy.9.wqkv_ref, bf16[4,384,384]{2,1,0:T(8,128)(2,1)} %bitcast.4, bf16[4,384,1536]{2,1,0:T(8,128)(2,1)} %wup_ref.1, ...), custom_call_target="tpu_custom_call" | custom-call | tf_op jit(solution)/shard_map/stack/pallas_call | solution.py:185
  58.2 1.9 %reshape.15 = bf16[1,256,2,384]{3,2,1,0:T(2,128)(2,1)} reshape(bf16[128,4,384]{2,1,0:T(4,128)(2,1)} %stack.1) | data formatting | bytes 786432 | tf_op jit(solution)/shard_map/reshape | solution.py:213

commit v2 on v1

--- a/solution.py
+++ b/solution.py
@@ -63,7 +63,7 @@
 
 
 def stack_kernel(x_ref, tab_ref, norms_ref, wqkv_ref, wout_ref, wup_ref, wdown_ref, y_ref,
-                 xv, wqkv, wout, wup, wdown, f_in, f_out, qkv_s, o_s, hid_s, zsend, recv,
+                 xv, wqkv, wout, wup, wdown, f_in, f_out, a_s, qkv_s, o_s, hid_s, zfin, zsend, recv,
                  x_sem, w_sem, send_sem, recv_sem, y_sem):
     me = lax.axis_index('sp')
     digits = (me // 32, (me // 8) % 4, (me // 2) % 4, me % 2)
@@ -110,7 +110,7 @@
             for b in range(2):
                 put(f_in, c * ROWS + 2 * a + b, rows[b * SLOTS:(b + 1) * SLOTS])
 
-    low = lax.broadcasted_iota(jnp.int32, (HALF, 128), 1) < 64
+    low = lax.broadcasted_iota(jnp.int32, (2 * DEV, 128), 1) < 64
 
     def load_rows(c):
         return jnp.concatenate([take(f_in, c * ROWS + 2 * j + i) for j in range(2) for i in range(2)], axis=0)
@@ -127,29 +127,31 @@
                 rows = recv[l - 1, c * SLOTS:(c + 1) * SLOTS].reshape(ROWS, D).astype(F32)
                 for t in range(3):
                     f_in[t, c * ROWS:(c + 1) * ROWS, :] = rows[:, t * 128:(t + 1) * 128]
-            if c == 0:
-                w_copies[l][0].wait()
             normed = layer_norm(load_rows(c), gains[0:1], gains[1:2])
-            proj = dot(normed, wqkv[l]).astype(BF)
             for j in range(2):
-                qkv_s[j, c * HALF:(c + 1) * HALF, :] = proj[j * HALF:(j + 1) * HALF]
+                a_s[j, c * HALF:(c + 1) * HALF, :] = normed[j * HALF:(j + 1) * HALF]
+        w_copies[l][0].wait()
+        normed = a_s[...].reshape(4 * DEV, D)
+        for n in range(0, QKV, 384):
+            proj = lax.dot_general(normed, wqkv[l, n:n + 384], (((1,), (1,)), ((), ())), preferred_element_type=F32)
+            qkv_s[:, :, n:n + 384] = proj.astype(BF).reshape(2, 2 * DEV, 384)
+        for j in range(2):
+            for t in range(3):
+                q = qkv_s[j, :, t * 128:(t + 1) * 128]
+                k = qkv_s[j, :, D + t * 128:D + (t + 1) * 128]
+                v = qkv_s[j, :, 2 * D + t * 128:2 * D + (t + 1) * 128]
+                zero = jnp.zeros_like(q)
+                qq = jnp.concatenate([jnp.where(low, q, zero), jnp.where(low, zero, q)], axis=0)
+                s = lax.dot_general(qq, k, (((1,), (1,)), ((), ())), preferred_element_type=F32)
+                e = jnp.exp2((s - jnp.max(s, axis=-1, keepdims=True)) * EXP_SCALE)
+                p = (e * (1.0 / jnp.sum(e, axis=-1, keepdims=True))).astype(BF)
+                oo = dot(p, v)
+                o_s[j, :, t * 128:(t + 1) * 128] = jnp.where(low, oo[:2 * DEV], oo[2 * DEV:]).astype(BF)
         for c in range(CHUNKS):
-            for j in range(2):
-                for t in range(3):
-                    q = qkv_s[j, c * HALF:(c + 1) * HALF, t * 128:(t + 1) * 128]
-                    k = qkv_s[j, :, D + t * 128:D + (t + 1) * 128]
-                    v = qkv_s[j, :, 2 * D + t * 128:2 * D + (t + 1) * 128]
-                    zero = jnp.zeros_like(q)
-                    qq = jnp.concatenate([jnp.where(low, q, zero), jnp.where(low, zero, q)], axis=0)
-                    s = lax.dot_general(qq, k, (((1,), (1,)), ((), ())), preferred_element_type=F32)
-                    e = jnp.exp2((s - jnp.max(s, axis=-1, keepdims=True)) * EXP_SCALE)
-                    p = (e * (1.0 / jnp.sum(e, axis=-1, keepdims=True))).astype(BF)
-                    oo = dot(p, v)
-                    o_s[j * HALF:(j + 1) * HALF, t * 128:(t + 1) * 128] = jnp.where(low, oo[:HALF], oo[HALF:]).astype(BF)
             if c == 0:
                 for cp in w_copies[l][1:]:
                     cp.wait()
-            h = (load_rows(c) + dot(o_s[...], wout[l])).astype(BF).astype(F32)
+            h = (load_rows(c) + dot(o_s[:, c * HALF:(c + 1) * HALF, :].reshape(ROWS, D), wout[l])).astype(BF).astype(F32)
             normed = layer_norm(h, gains[2:3], gains[3:4])
             for n in range(0, HID, 512):
                 hid_s[:, n:n + 512] = gelu(dot(normed, wup[l, :, n:n + 512])).astype(BF)
@@ -158,12 +160,15 @@
                 for b in range(2):
                     put(f_out, 2 * b + j, z[(2 * j + b) * SLOTS:(2 * j + b + 1) * SLOTS])
             zs = jnp.concatenate([f_out[t] for t in range(3)], axis=1)
-            zsend[l, c * SLOTS:(c + 1) * SLOTS] = zs.astype(BF).reshape(SLOTS, 4, D)
+            if l == BLOCKS - 1:
+                zfin[c * SLOTS:(c + 1) * SLOTS] = zs.astype(BF).reshape(SLOTS, 2, 2, D)
+            else:
+                zsend[l, c * SLOTS:(c + 1) * SLOTS] = zs.astype(BF).reshape(SLOTS, 4, D)
             if l == 0 and c == 0:
                 pl.semaphore_wait(barrier, DEV - 1)
             for k in range(c * SLOTS, (c + 1) * SLOTS):
                 if l == BLOCKS - 1:
-                    pltpu.make_async_copy(zsend.at[l, k], y_ref.at[dev_of(k)], y_sem).start()
+                    pltpu.make_async_copy(zfin.at[k], y_ref.at[dev_of(k)], y_sem).start()
                 elif k < DEV - 1:
                     pltpu.make_async_remote_copy(zsend.at[l, k], recv.at[l, BACK[k]], send_sem.at[l, c], recv_sem.at[l, c],
                                                  device_id={'sp': dev_of(k)}, device_id_type=pl.DeviceIdType.MESH).start()
@@ -173,7 +178,7 @@
             n = SLOTS - (c == CHUNKS - 1)
             sent = zsend.at[l, pl.ds(c * SLOTS, n)]
             pltpu.make_async_copy(sent, sent, send_sem.at[l, c]).wait()
-    pltpu.make_async_copy(zsend.at[BLOCKS - 1], y_ref, y_sem).wait()
+    pltpu.make_async_copy(zfin, y_ref, y_sem).wait()
 
 
 def solution(mesh):
@@ -184,21 +189,23 @@
         vmem = pl.BlockSpec(memory_space=pltpu.VMEM)
         out = pl.pallas_call(
             stack_kernel,
-            out_shape=jax.ShapeDtypeStruct((DEV, 4, D), BF),
+            out_shape=jax.ShapeDtypeStruct((DEV, 2, 2, D), BF),
             in_specs=[anywhere, vmem, vmem, anywhere, anywhere, anywhere, anywhere],
             out_specs=anywhere,
             scratch_shapes=[
                 pltpu.VMEM((2, 2 * DEV, D), BF),
-                pltpu.VMEM((BLOCKS, D, QKV), BF),
+                pltpu.VMEM((BLOCKS, QKV, D), BF),
                 pltpu.VMEM((BLOCKS, D, D), BF),
                 pltpu.VMEM((BLOCKS, D, HID), BF),
                 pltpu.VMEM((BLOCKS, HID, D), BF),
                 pltpu.VMEM((3, 4 * DEV, 128), F32),
                 pltpu.VMEM((3, ROWS, 128), F32),
+                pltpu.VMEM((2, 2 * DEV, D), BF),
                 pltpu.VMEM((2, 2 * DEV, QKV), BF),
-                pltpu.VMEM((ROWS, D), BF),
+                pltpu.VMEM((2, 2 * DEV, D), BF),
                 pltpu.VMEM((ROWS, HID), BF),
-                pltpu.VMEM((BLOCKS, DEV, 4, D), BF),
+                pltpu.VMEM((DEV, 2, 2, D), BF),
+                pltpu.VMEM((BLOCKS - 1, DEV, 4, D), BF),
                 pltpu.VMEM((BLOCKS - 1, DEV, 4, D), BF),
                 pltpu.SemaphoreType.DMA,
                 pltpu.SemaphoreType.DMA((BLOCKS, 4)),
@@ -208,7 +215,7 @@
             ],
             compiler_params=pltpu.CompilerParams(collective_id=0, has_side_effects=True, vmem_limit_bytes=60 * 1024 * 1024),
             name='stack',
-        )(latents.reshape(2, 2 * DEV, D), jnp.asarray(table, jnp.int32), norms, w_qkv.reshape(BLOCKS, D, QKV),
+        )(latents.reshape(2, 2 * DEV, D), jnp.asarray(table, jnp.int32), norms, jnp.transpose(w_qkv, (0, 2, 3, 4, 1)).reshape(BLOCKS, QKV, D),
           w_out.reshape(BLOCKS, D, D), w_up, w_down)
         return out.reshape(1, 2 * DEV, 2, D)
 

time: 60.5 us -> 57.5 us (0.950)
  local copies, waits for them, and re-layouts: 7.69 us -> 2.01 us
  Pallas kernels: 52.4 us -> 55.4 us
    reshape x2 -> x0, local copies, waits for them, and re-layouts: 7.69 us -> none  [the longest x1 5.77 us: local_stack(): w_qkv.reshape(BLOCKS, D, QKV)]
    pallas_call x1, Pallas kernels: 52.4 us -> 55.4 us  [local_stack(): pl.pallas_call(stack_kernel, out_shape=jax.ShapeDtypeStruct((DEV, 2, 2, D...]
    unnamed x0 -> x1, local copies, waits for them, and re-layouts: none -> 2.01 us
where the time goes in v2:
time: 57.5 us; the launch traced here: 57.4 us
  Pallas kernels  55.4 us (96%)
  local copies, waits for them, and re-layouts  2.01 us (3%)
    pallas_call x1, Pallas kernels, local_stack(): pl.pallas_call(stack_kernel, out_shape=jax.ShapeDtypeStruct((DEV, 2, 2, D...  55.4 us
    unnamed x1, local copies, waits for them, and re-layouts  2.01 us

profile of v2, /device:TPU:1, one launch (start us, length us, event | category | flops | bytes accessed | tf_op | source)
XLA Modules:
  0.0 57.4 jit_solution(6155889876918779992)
XLA Ops:
  0.0 55.4 %stack.1 = bf16[128,2,2,384]{3,2,1,0:T(2,128)(2,1)} custom-call(bf16[2,256,384]{2,1,0:T(8,128)(2,1)} %bitcast.9, s32[2,128,5]{2,1,0:T(8,128)} %constant.2.clone.tab_ref, f32[4,4,384]{2,1,0:T(4,128)} %norms_ref.1, bf16[4,1152,384]{2,1,0:T(8,128)(2,1)} %bitcast.6, bf16[4,384,384]{2,1,0:T(8,128)(2,1)} %bitcast.8, bf16[4,384,1536]{2,1,0:T(8,128)(2,1)} %wup_ref.1, ...), custom_call_target="tpu_custom_call" | custom-call | tf_op jit(solution)/shard_map/stack/pallas_call | solution.py:190
  55.4 2.0 %copy.9 = bf16[1,256,2,384]{3,2,1,0:T(2,128)(2,1)} copy(bf16[1,256,2,384]{3,2,1,0:T(2,128)(2,1)} %bitcast.7) | data formatting | bytes 786432

commit v3 on v2

v3 whole, which is shorter than its diff:
```python
import math

import jax
import jax.numpy as jnp
from jax import lax
from jax.experimental import pallas as pl
from jax.experimental.pallas import tpu as pltpu
from jax.sharding import PartitionSpec as P

EPS = 1e-6
D = 384
QKV = 3 * D
HID = 4 * D
DEV = 128
SEQ = 2 * DEV
BLOCKS = 4
CUTS = (0, 64, 128)
CHUNKS = tuple((a, b - a) for a, b in zip(CUTS, CUTS[1:]))
BIG = max(n for _, n in CHUNKS)
UP = 256
EXP_SCALE = 64 ** -0.5 * math.log2(math.e)
GELU_A = math.sqrt(2.0 / math.pi)
GELU_B = GELU_A * 0.044715
BF = jnp.bfloat16
F32 = jnp.float32


def slot_table():
    hops = (0, 1, 2, 1)
    offs = [(z, y, x, c) for z in range(4) for y in range(4) for x in range(4) for c in range(2)]

    def opposite(o):
        return (-o[0]) % 4, (-o[1]) % 4, (-o[2]) % 4, o[3]

    offs.sort(key=lambda o: (-(hops[o[0]] + hops[o[1]] + hops[o[2]]), -o[3], min(o, opposite(o)), o))
    index = {o: k for k, o in enumerate(offs)}
    back = [index[opposite(o)] for o in offs]
    assert all(start <= back[k] < start + n for start, n in CHUNKS for k in range(start, start + n))
    return offs, back


OFFS, BACK = slot_table()


def layer_norm(u, gain, shift):
    mean = jnp.mean(u, axis=-1, keepdims=True)
    cen = u - mean
    var = jnp.mean(cen * cen, axis=-1, keepdims=True)
    return (cen * lax.rsqrt(var + EPS) * gain + shift).astype(BF)


def gelu(x):
    half = 0.5 * x
    return half + half * jnp.tanh(x * (GELU_A + GELU_B * (x * x)))


def dot(a, b):
    return jnp.dot(a, b, preferred_element_type=F32)


def dot_t(a, b):
    return lax.dot_general(a, b, (((1,), (1,)), ((), ())), preferred_element_type=F32)


def put(ref, start, rows):
    n = rows.shape[0]
    for t in range(3):
        ref[t, pl.ds(start, n, stride=4), :] = rows[:, t * 128:(t + 1) * 128]


def take(ref, start, n):
    return jnp.concatenate([ref[t, pl.ds(start, n, stride=4), :] for t in range(3)], axis=1)


def stack_kernel(x_ref, tab_ref, norms_ref, wqkv_ref, wout_ref, wup_ref, wdown_ref, y_ref,
                 xv, tab, norms, wqkv, wout, wup, wdown, f_in, f_out, a_s, qkv_s, o_s, hid_s, zfin, zsend, recv,
                 in_sem, w_sem, send_sem, recv_sem, y_sem):
    me = lax.axis_index('sp')
    digits = (me // 32, (me // 8) % 4, (me // 2) % 4, me % 2)
    barrier = pltpu.get_barrier_semaphore()

    def greet(i, carry):
        pl.semaphore_signal(barrier, inc=1, device_id={'sp': lax.rem(me + i, DEV)}, device_id_type=pl.DeviceIdType.MESH)
        return carry

    first = [pltpu.make_async_copy(src, dst, in_sem.at[i]) for i, (src, dst) in enumerate(((x_ref, xv), (tab_ref, tab), (norms_ref, norms)))]
    weights = [[pltpu.make_async_copy(src.at[l], dst.at[l], w_sem.at[l, i])
                for i, (src, dst) in enumerate(((wqkv_ref, wqkv), (wout_ref, wout), (wup_ref, wup), (wdown_ref, wdown)))]
               for l in range(BLOCKS)]
    for cp in first:
        cp.start()
    weights[0][0].start()
    lax.fori_loop(1, DEV, greet, 0)

    zpos = [(((digits[0] - d) + 4) % 4) * 32 for d in range(4)]
    ypos = [(((digits[1] - d) + 4) % 4) * 8 for d in range(4)]
    xpos = [(((digits[2] - d) + 4) % 4) * 2 for d in range(4)]
    cpos = [(digits[3] + d) % 2 for d in range(2)]

    def dev_of(k):
        o = OFFS[k]
        return zpos[o[0]] + ypos[o[1]] + xpos[o[2]] + cpos[o[3]]

    def send(l, c, k):
        if l == BLOCKS - 1:
            pltpu.make_async_copy(zfin.at[k], y_ref.at[dev_of(k)], y_sem).start()
        elif k < DEV - 1:
            pltpu.make_async_remote_copy(zsend.at[l, k], recv.at[l, BACK[k]], send_sem.at[l, c], recv_sem.at[l, c],
                                         device_id={'sp': dev_of(k)}, device_id_type=pl.DeviceIdType.MESH).start()

    def load_rows(c):
        start, n = CHUNKS[c]
        return jnp.concatenate([take(f_in, 4 * start + 2 * j + i, n) for j in range(2) for i in range(2)], axis=0)

    for cp in first:
        cp.wait()
    for cp in weights[0][1:]:
        cp.start()
    lane = lax.broadcasted_iota(jnp.int32, (SEQ, SEQ), 1)
    dz = (digits[0] - tab[:, 0:1] + 4) % 4
    dy = (digits[1] - tab[:, 1:2] + 4) % 4
    dx = (digits[2] - tab[:, 2:3] + 4) % 4
    dc = (digits[3] + tab[:, 3:4]) % 2
    patch = 2 * (dz * 32 + dy * 8 + dx * 2 + dc) + tab[:, 4:5]
    pick = jnp.where(lane == patch, 1.0, 0.0).astype(BF)
    for a in range(2):
        rows = dot(pick, xv[a])
        for start, n in CHUNKS:
            for b in range(2):
                put(f_in, 4 * start + 2 * a + b, rows[2 * start + b * n:2 * start + (b + 1) * n])

    low = lax.broadcasted_iota(jnp.int32, (SEQ, 128), 1) < 64

    for l in range(BLOCKS):
        gains = norms[l]
        for c, (start, n) in enumerate(CHUNKS):
            if l > 0:
                last = start + n == DEV
                got = recv.at[l - 1, pl.ds(start, n - last)]
                pltpu.make_async_copy(got, got, recv_sem.at[l - 1, c]).wait()
                if last:
                    recv[l - 1, DEV - 1] = zsend[l - 1, DEV - 1]
                rows = recv[l - 1, start:start + n].reshape(4 * n, D).astype(F32)
                for t in range(3):
                    f_in[t, 4 * start:4 * (start + n), :] = rows[:, t * 128:(t + 1) * 128]
            normed = layer_norm(load_rows(c), gains[0:1], gains[1:2])
            for j in range(2):
                a_s[j, 2 * start:2 * (start + n), :] = normed[2 * j * n:2 * (j + 1) * n]
        weights[l][0].wait()
        normed = a_s[...].reshape(2 * SEQ, D)
        for m in range(0, QKV, 384):
            qkv_s[:, :, m:m + 384] = dot_t(normed, wqkv[l, m:m + 384]).astype(BF).reshape(2, SEQ, 384)
        if l == 0:
            for row in weights[1:]:
                for cp in row:
                    cp.start()
        for j in range(2):
            for t in range(3):
                q = qkv_s[j, :, t * 128:(t + 1) * 128]
                k = qkv_s[j, :, D + t * 128:D + (t + 1) * 128]
                v = qkv_s[j, :, 2 * D + t * 128:2 * D + (t + 1) * 128]
                zero = jnp.zeros_like(q)
                s = dot_t(jnp.concatenate([jnp.where(low, q, zero), jnp.where(low, zero, q)], axis=0), k)
                e = jnp.exp2((s - jnp.max(s, axis=-1, keepdims=True)) * EXP_SCALE)
                p = (e * (1.0 / jnp.sum(e, axis=-1, keepdims=True))).astype(BF)
                oo = dot(p, v)
                o_s[j, :, t * 128:(t + 1) * 128] = jnp.where(low, oo[:SEQ], oo[SEQ:]).astype(BF)
        for cp in weights[l][1:]:
            cp.wait()
        pending = []

        def flush(count):
            for args in pending[:count]:
                send(*args)
            del pending[:count]

        for c, (start, n) in enumerate(CHUNKS):
            share = -(-len(pending) // 7)
            mixed = jnp.concatenate([o_s[j, 2 * start:2 * (start + n), :] for j in range(2)], axis=0)
            h = (load_rows(c) + dot(mixed, wout[l])).astype(BF).astype(F32)
            normed = layer_norm(h, gains[2:3], gains[3:4])
            for m in range(0, HID, UP):
                flush(share)
                hid_s[0:4 * n, m:m + UP] = gelu(dot(normed, wup[l, :, m:m + UP])).astype(BF)
            flush(len(pending))
            z = h + dot(hid_s[0:4 * n], wdown[l])
            for j in range(2):
                for b in range(2):
                    put(f_out, 2 * b + j, z[(2 * j + b) * n:(2 * j + b + 1) * n])
            zs = jnp.concatenate([f_out[t, 0:4 * n] for t in range(3)], axis=1).astype(BF)
            if l == BLOCKS - 1:
                zfin[start:start + n] = zs.reshape(n, 2, 2, D)
            else:
                zsend[l, start:start + n] = zs.reshape(n, 4, D)
            if l == 0 and c == 0:
                pl.semaphore_wait(barrier, DEV - 1)
            pending = [(l, c, k) for k in range(start, start + n)]
        flush(len(pending))

    for l in range(BLOCKS - 1):
        for c, (start, n) in enumerate(CHUNKS):
            sent = zsend.at[l, pl.ds(start, n - (start + n == DEV))]
            pltpu.make_async_copy(sent, sent, send_sem.at[l, c]).wait()
    pltpu.make_async_copy(zfin, y_ref, y_sem).wait()


def solution(mesh):
    table = [list(OFFS[start + r]) + [b] for start, n in CHUNKS for b in range(2) for r in range(n)]

    def local_stack(latents, norms, w_qkv, w_out, w_up, w_down):
        anywhere = pl.BlockSpec(memory_space=pl.ANY)
        dma = pltpu.SemaphoreType.DMA
        out = pl.pallas_call(
            stack_kernel,
            out_shape=jax.ShapeDtypeStruct((DEV, 2, 2, D), BF),
            in_specs=[anywhere] * 7,
            out_specs=anywhere,
            scratch_shapes=[
                pltpu.VMEM((2, SEQ, D), BF),
                pltpu.VMEM((SEQ, 5), jnp.int32),
                pltpu.VMEM((BLOCKS, 4, D), F32),
                pltpu.VMEM((BLOCKS, QKV, D), BF),
                pltpu.VMEM((BLOCKS, D, D), BF),
                pltpu.VMEM((BLOCKS, D, HID), BF),
                pltpu.VMEM((BLOCKS, HID, D), BF),
                pltpu.VMEM((3, 2 * SEQ, 128), F32),
                pltpu.VMEM((3, 4 * BIG, 128), F32),
                pltpu.VMEM((2, SEQ, D), BF),
                pltpu.VMEM((2, SEQ, QKV), BF),
                pltpu.VMEM((2, SEQ, D), BF),
                pltpu.VMEM((4 * BIG, HID), BF),
                pltpu.VMEM((DEV, 2, 2, D), BF),
                pltpu.VMEM((BLOCKS - 1, DEV, 4, D), BF),
                pltpu.VMEM((BLOCKS - 1, DEV, 4, D), BF),
                dma((3,)),
                dma((BLOCKS, 4)),
                dma((BLOCKS - 1, len(CHUNKS))),
                dma((BLOCKS - 1, len(CHUNKS))),
                dma,
            ],
            compiler_params=pltpu.CompilerParams(collective_id=0, has_side_effects=True, vmem_limit_bytes=60 * 1024 * 1024),
            name='stack',
        )(latents.reshape(2, SEQ, D), jnp.asarray(table, jnp.int32), norms, jnp.transpose(w_qkv, (0, 2, 3, 4, 1)).reshape(BLOCKS, QKV, D),
          w_out.reshape(BLOCKS, D, D), w_up, w_down)
        return out.reshape(1, SEQ, 2, D)

    replicated = P()
    return jax.shard_map(local_stack, mesh=mesh, in_specs=(P('data', 'sp', None, None), replicated, replicated, replicated, replicated, replicated), out_specs=P('data', None, 'sp', None), check_vma=False)
```

time: 57.5 us -> 53.7 us (0.934)
  Pallas kernels: 55.4 us -> 51.5 us
    pallas_call x1, Pallas kernels: 55.4 us -> 51.5 us  [local_stack(): pl.pallas_call(stack_kernel, out_shape=jax.ShapeDtypeStruct((DEV, 2, 2, D...]
where the time goes in v3:
time: 53.7 us; the launch traced here: 53.5 us
  Pallas kernels  51.5 us (96%)
  local copies, waits for them, and re-layouts  2.01 us (4%)
    pallas_call x1, Pallas kernels, local_stack(): pl.pallas_call(stack_kernel, out_shape=jax.ShapeDtypeStruct((DEV, 2, 2, D...  51.5 us
    unnamed x1, local copies, waits for them, and re-layouts  2.01 us

profile of v3, /device:TPU:1, one launch (start us, length us, event | category | flops | bytes accessed | tf_op | source)
XLA Modules:
  0.0 53.5 jit_solution(1122513831362783464)
XLA Ops:
  0.0 51.5 %stack.1 = bf16[128,2,2,384]{3,2,1,0:T(2,128)(2,1)} custom-call(bf16[2,256,384]{2,1,0:T(8,128)(2,1)} %bitcast.9, s32[256,5]{1,0:T(8,128)} %constant.2.clone.tab_ref, f32[4,4,384]{2,1,0:T(4,128)} %norms_ref.1, bf16[4,1152,384]{2,1,0:T(8,128)(2,1)} %bitcast.6, bf16[4,384,384]{2,1,0:T(8,128)(2,1)} %bitcast.8, bf16[4,384,1536]{2,1,0:T(8,128)(2,1)} %wup_ref.1, ...), custom_call_target="tpu_custom_call" | custom-call | tf_op jit(solution)/shard_map/stack/pallas_call | solution.py:213
  51.5 2.0 %copy.9 = bf16[1,256,2,384]{3,2,1,0:T(2,128)(2,1)} copy(bf16[1,256,2,384]{3,2,1,0:T(2,128)(2,1)} %bitcast.7) | data formatting | bytes 786432

commit v4 on v3

--- a/solution.py
+++ b/solution.py
@@ -17,7 +17,7 @@
 CUTS = (0, 64, 128)
 CHUNKS = tuple((a, b - a) for a, b in zip(CUTS, CUTS[1:]))
 BIG = max(n for _, n in CHUNKS)
-UP = 256
+UP = 512
 EXP_SCALE = 64 ** -0.5 * math.log2(math.e)
 GELU_A = math.sqrt(2.0 / math.pi)
 GELU_B = GELU_A * 0.044715
@@ -73,7 +73,7 @@
 
 
 def stack_kernel(x_ref, tab_ref, norms_ref, wqkv_ref, wout_ref, wup_ref, wdown_ref, y_ref,
-                 xv, tab, norms, wqkv, wout, wup, wdown, f_in, f_out, a_s, qkv_s, o_s, hid_s, zfin, zsend, recv,
+                 xv, tab, norms, wqkv, wout, wup, wdown, wq_s, f_in, f_out, a_s, qkv_s, o_s, hid_s, zfin, zsend, recv,
                  in_sem, w_sem, send_sem, recv_sem, y_sem):
     me = lax.axis_index('sp')
     digits = (me // 32, (me // 8) % 4, (me // 2) % 4, me % 2)
@@ -129,8 +129,19 @@
             for b in range(2):
                 put(f_in, 4 * start + 2 * a + b, rows[2 * start + b * n:2 * start + (b + 1) * n])
 
-    low = lax.broadcasted_iota(jnp.int32, (SEQ, 128), 1) < 64
-
+    pending = []
+
+    def flush(count):
+        for args in pending[:count]:
+            send(*args)
+        del pending[:count]
+
+    def lay_out(l):
+        for m in range(0, QKV, 384):
+            wq_s[:, m:m + 384] = wqkv[l, m:m + 384].T
+
+    weights[0][0].wait()
+    lay_out(0)
     for l in range(BLOCKS):
         gains = norms[l]
         for c, (start, n) in enumerate(CHUNKS):
@@ -146,43 +157,38 @@
             normed = layer_norm(load_rows(c), gains[0:1], gains[1:2])
             for j in range(2):
                 a_s[j, 2 * start:2 * (start + n), :] = normed[2 * j * n:2 * (j + 1) * n]
-        weights[l][0].wait()
-        normed = a_s[...].reshape(2 * SEQ, D)
-        for m in range(0, QKV, 384):
-            qkv_s[:, :, m:m + 384] = dot_t(normed, wqkv[l, m:m + 384]).astype(BF).reshape(2, SEQ, 384)
+            if (start + n) % 64 == 0:
+                r = 2 * (start + n) - 128
+                normed = a_s[:, r:r + 128].reshape(256, D)
+                for m in range(0, QKV, 384):
+                    qkv_s[:, r:r + 128, m:m + 384] = dot(normed, wq_s[:, m:m + 384]).astype(BF).reshape(2, 128, 384)
         if l == 0:
             for row in weights[1:]:
                 for cp in row:
                     cp.start()
-        for j in range(2):
-            for t in range(3):
-                q = qkv_s[j, :, t * 128:(t + 1) * 128]
-                k = qkv_s[j, :, D + t * 128:D + (t + 1) * 128]
-                v = qkv_s[j, :, 2 * D + t * 128:2 * D + (t + 1) * 128]
-                zero = jnp.zeros_like(q)
-                s = dot_t(jnp.concatenate([jnp.where(low, q, zero), jnp.where(low, zero, q)], axis=0), k)
-                e = jnp.exp2((s - jnp.max(s, axis=-1, keepdims=True)) * EXP_SCALE)
-                p = (e * (1.0 / jnp.sum(e, axis=-1, keepdims=True))).astype(BF)
-                oo = dot(p, v)
-                o_s[j, :, t * 128:(t + 1) * 128] = jnp.where(low, oo[:SEQ], oo[SEQ:]).astype(BF)
-        for cp in weights[l][1:]:
-            cp.wait()
-        pending = []
-
-        def flush(count):
-            for args in pending[:count]:
-                send(*args)
-            del pending[:count]
-
         for c, (start, n) in enumerate(CHUNKS):
-            share = -(-len(pending) // 7)
-            mixed = jnp.concatenate([o_s[j, 2 * start:2 * (start + n), :] for j in range(2)], axis=0)
-            h = (load_rows(c) + dot(mixed, wout[l])).astype(BF).astype(F32)
+            low = lax.broadcasted_iota(jnp.int32, (2 * n, 128), 1) < 64
+            share = len(pending)
+            for j in range(2):
+                for t in range(3):
+                    flush(share)
+                    q = qkv_s[j, 2 * start:2 * (start + n), t * 128:(t + 1) * 128]
+                    k = qkv_s[j, :, D + t * 128:D + (t + 1) * 128]
+                    v = qkv_s[j, :, 2 * D + t * 128:2 * D + (t + 1) * 128]
+                    zero = jnp.zeros_like(q)
+                    s = dot_t(jnp.concatenate([jnp.where(low, q, zero), jnp.where(low, zero, q)], axis=0), k)
+                    e = jnp.exp2((s - jnp.max(s, axis=-1, keepdims=True)) * EXP_SCALE)
+                    p = (e * (1.0 / jnp.sum(e, axis=-1, keepdims=True))).astype(BF)
+                    oo = dot(p, v)
+                    o_s[2 * j * n:2 * (j + 1) * n, t * 128:(t + 1) * 128] = jnp.where(low, oo[:2 * n], oo[2 * n:]).astype(BF)
+            flush(len(pending))
+            if c == 0:
+                for cp in weights[l][1:]:
+                    cp.wait()
+            h = (load_rows(c) + dot(o_s[0:4 * n], wout[l])).astype(BF).astype(F32)
             normed = layer_norm(h, gains[2:3], gains[3:4])
             for m in range(0, HID, UP):
-                flush(share)
                 hid_s[0:4 * n, m:m + UP] = gelu(dot(normed, wup[l, :, m:m + UP])).astype(BF)
-            flush(len(pending))
             z = h + dot(hid_s[0:4 * n], wdown[l])
             for j in range(2):
                 for b in range(2):
@@ -194,8 +200,11 @@
                 zsend[l, start:start + n] = zs.reshape(n, 4, D)
             if l == 0 and c == 0:
                 pl.semaphore_wait(barrier, DEV - 1)
-            pending = [(l, c, k) for k in range(start, start + n)]
+            pending += [(l, c, k) for k in range(start, start + n)]
         flush(len(pending))
+        if l < BLOCKS - 1:
+            weights[l + 1][0].wait()
+            lay_out(l + 1)
 
     for l in range(BLOCKS - 1):
         for c, (start, n) in enumerate(CHUNKS):
@@ -223,11 +232,12 @@
                 pltpu.VMEM((BLOCKS, D, D), BF),
                 pltpu.VMEM((BLOCKS, D, HID), BF),
                 pltpu.VMEM((BLOCKS, HID, D), BF),
+                pltpu.VMEM((D, QKV), BF),
                 pltpu.VMEM((3, 2 * SEQ, 128), F32),
                 pltpu.VMEM((3, 4 * BIG, 128), F32),
                 pltpu.VMEM((2, SEQ, D), BF),
                 pltpu.VMEM((2, SEQ, QKV), BF),
-                pltpu.VMEM((2, SEQ, D), BF),
+                pltpu.VMEM((4 * BIG, D), BF),
                 pltpu.VMEM((4 * BIG, HID), BF),
                 pltpu.VMEM((DEV, 2, 2, D), BF),
                 pltpu.VMEM((BLOCKS - 1, DEV, 4, D), BF),

time: 53.7 us -> 51.1 us (0.952)
  Pallas kernels: 51.5 us -> 48.7 us
    pallas_call x1, Pallas kernels: 51.5 us -> 48.7 us  [local_stack(): pl.pallas_call(stack_kernel, out_shape=jax.ShapeDtypeStruct((DEV, 2, 2, D...]
where the time goes in v4:
time: 51.1 us; the launch traced here: 50.7 us
  Pallas kernels  48.7 us (95%)
  local copies, waits for them, and re-layouts  2.01 us (4%)
    pallas_call x1, Pallas kernels, local_stack(): pl.pallas_call(stack_kernel, out_shape=jax.ShapeDtypeStruct((DEV, 2, 2, D...  48.7 us
    unnamed x1, local copies, waits for them, and re-layouts  2.01 us

profile of v4, /device:TPU:1, one launch (start us, length us, event | category | flops | bytes accessed | tf_op | source)
XLA Modules:
  0.0 50.7 jit_solution(14361309551759384899)
XLA Ops:
  0.0 48.7 %stack.1 = bf16[128,2,2,384]{3,2,1,0:T(2,128)(2,1)} custom-call(bf16[2,256,384]{2,1,0:T(8,128)(2,1)} %bitcast.9, s32[256,5]{1,0:T(8,128)} %constant.2.clone.tab_ref, f32[4,4,384]{2,1,0:T(4,128)} %norms_ref.1, bf16[4,1152,384]{2,1,0:T(8,128)(2,1)} %bitcast.6, bf16[4,384,384]{2,1,0:T(8,128)(2,1)} %bitcast.8, bf16[4,384,1536]{2,1,0:T(8,128)(2,1)} %wup_ref.1, ...), custom_call_target="tpu_custom_call" | custom-call | tf_op jit(solution)/shard_map/stack/pallas_call | solution.py:222
  48.7 2.0 %copy.9 = bf16[1,256,2,384]{3,2,1,0:T(2,128)(2,1)} copy(bf16[1,256,2,384]{3,2,1,0:T(2,128)(2,1)} %bitcast.7) | data formatting | bytes 786432

commit v5 on v4

--- a/solution.py
+++ b/solution.py
@@ -14,10 +14,11 @@
 DEV = 128
 SEQ = 2 * DEV
 BLOCKS = 4
-CUTS = (0, 64, 128)
+CUTS = (0, 64, 96, 128)
 CHUNKS = tuple((a, b - a) for a, b in zip(CUTS, CUTS[1:]))
-BIG = max(n for _, n in CHUNKS)
+BIG = 64
 UP = 512
+HALVES = [[c for c, (start, n) in enumerate(CHUNKS) if start // 64 == half] for half in range(2)]
 EXP_SCALE = 64 ** -0.5 * math.log2(math.e)
 GELU_A = math.sqrt(2.0 / math.pi)
 GELU_B = GELU_A * 0.044715
@@ -166,13 +167,16 @@
             for row in weights[1:]:
                 for cp in row:
                     cp.start()
-        for c, (start, n) in enumerate(CHUNKS):
-            low = lax.broadcasted_iota(jnp.int32, (2 * n, 128), 1) < 64
-            share = len(pending)
+        if l == BLOCKS - 1:
+            plan = [(0, SEQ, (HALVES[0], HALVES[1]))]
+        else:
+            plan = [(0, 128, (HALVES[0],)), (128, 128, tuple((c,) for c in HALVES[1]))]
+        for base, size, steps in plan:
+            low = lax.broadcasted_iota(jnp.int32, (size, 128), 1) < 64
+            flush(len(pending))
             for j in range(2):
                 for t in range(3):
-                    flush(share)
-                    q = qkv_s[j, 2 * start:2 * (start + n), t * 128:(t + 1) * 128]
+                    q = qkv_s[j, base:base + size, t * 128:(t + 1) * 128]
                     k = qkv_s[j, :, D + t * 128:D + (t + 1) * 128]
                     v = qkv_s[j, :, 2 * D + t * 128:2 * D + (t + 1) * 128]
                     zero = jnp.zeros_like(q)
@@ -180,27 +184,35 @@
                     e = jnp.exp2((s - jnp.max(s, axis=-1, keepdims=True)) * EXP_SCALE)
                     p = (e * (1.0 / jnp.sum(e, axis=-1, keepdims=True))).astype(BF)
                     oo = dot(p, v)
-                    o_s[2 * j * n:2 * (j + 1) * n, t * 128:(t + 1) * 128] = jnp.where(low, oo[:2 * n], oo[2 * n:]).astype(BF)
-            flush(len(pending))
-            if c == 0:
+                    o_s[j, base:base + size, t * 128:(t + 1) * 128] = jnp.where(low, oo[:size], oo[size:]).astype(BF)
+            if base == 0:
                 for cp in weights[l][1:]:
                     cp.wait()
-            h = (load_rows(c) + dot(o_s[0:4 * n], wout[l])).astype(BF).astype(F32)
-            normed = layer_norm(h, gains[2:3], gains[3:4])
-            for m in range(0, HID, UP):
-                hid_s[0:4 * n, m:m + UP] = gelu(dot(normed, wup[l, :, m:m + UP])).astype(BF)
-            z = h + dot(hid_s[0:4 * n], wdown[l])
-            for j in range(2):
-                for b in range(2):
-                    put(f_out, 2 * b + j, z[(2 * j + b) * n:(2 * j + b + 1) * n])
-            zs = jnp.concatenate([f_out[t, 0:4 * n] for t in range(3)], axis=1).astype(BF)
-            if l == BLOCKS - 1:
-                zfin[start:start + n] = zs.reshape(n, 2, 2, D)
-            else:
-                zsend[l, start:start + n] = zs.reshape(n, 4, D)
-            if l == 0 and c == 0:
-                pl.semaphore_wait(barrier, DEV - 1)
-            pending += [(l, c, k) for k in range(start, start + n)]
+            for step in steps:
+                pieces = [CHUNKS[c] for c in step]
+                total = sum(4 * n for _, n in pieces)
+                mixed = jnp.concatenate([o_s[j, 2 * start:2 * (start + n), :] for start, n in pieces for j in range(2)], axis=0)
+                h = (jnp.concatenate([load_rows(c) for c in step], axis=0) + dot(mixed, wout[l])).astype(BF).astype(F32)
+                normed = layer_norm(h, gains[2:3], gains[3:4])
+                flush(len(pending))
+                for m in range(0, HID, UP):
+                    hid_s[0:total, m:m + UP] = gelu(dot(normed, wup[l, :, m:m + UP])).astype(BF)
+                z = h + dot(hid_s[0:total], wdown[l])
+                row = 0
+                for c in step:
+                    start, n = CHUNKS[c]
+                    for j in range(2):
+                        for b in range(2):
+                            put(f_out, 2 * b + j, z[row:row + n])
+                            row += n
+                    zs = jnp.concatenate([f_out[t, 0:4 * n] for t in range(3)], axis=1).astype(BF)
+                    if l == BLOCKS - 1:
+                        zfin[start:start + n] = zs.reshape(n, 2, 2, D)
+                    else:
+                        zsend[l, start:start + n] = zs.reshape(n, 4, D)
+                    pending += [(l, c, k) for k in range(start, start + n)]
+                if l == 0 and base == 0:
+                    pl.semaphore_wait(barrier, DEV - 1)
         flush(len(pending))
         if l < BLOCKS - 1:
             weights[l + 1][0].wait()
@@ -237,7 +249,7 @@
                 pltpu.VMEM((3, 4 * BIG, 128), F32),
                 pltpu.VMEM((2, SEQ, D), BF),
                 pltpu.VMEM((2, SEQ, QKV), BF),
-                pltpu.VMEM((4 * BIG, D), BF),
+                pltpu.VMEM((2, SEQ, D), BF),
                 pltpu.VMEM((4 * BIG, HID), BF),
                 pltpu.VMEM((DEV, 2, 2, D), BF),
                 pltpu.VMEM((BLOCKS - 1, DEV, 4, D), BF),

time: 51.1 us -> 50.6 us (level)
  no operation moved by 1% of the time
where the time goes in v5:
time: 50.6 us; the launch traced here: 50.4 us
  Pallas kernels  48.4 us (96%)
  local copies, waits for them, and re-layouts  2.01 us (4%)
    pallas_call x1, Pallas kernels, local_stack(): pl.pallas_call(stack_kernel, out_shape=jax.ShapeDtypeStruct((DEV, 2, 2, D...  48.4 us
    unnamed x1, local copies, waits for them, and re-layouts  2.01 us

profile of v5, /device:TPU:1, one launch (start us, length us, event | category | flops | bytes accessed | tf_op | source)
XLA Modules:
  0.0 50.4 jit_solution(11653233859074594308)
XLA Ops:
  0.0 48.4 %stack.1 = bf16[128,2,2,384]{3,2,1,0:T(2,128)(2,1)} custom-call(bf16[2,256,384]{2,1,0:T(8,128)(2,1)} %bitcast.9, s32[256,5]{1,0:T(8,128)} %constant.2.clone.tab_ref, f32[4,4,384]{2,1,0:T(4,128)} %norms_ref.1, bf16[4,1152,384]{2,1,0:T(8,128)(2,1)} %bitcast.6, bf16[4,384,384]{2,1,0:T(8,128)(2,1)} %bitcast.8, bf16[4,384,1536]{2,1,0:T(8,128)(2,1)} %wup_ref.1, ...), custom_call_target="tpu_custom_call" | custom-call | tf_op jit(solution)/shard_map/stack/pallas_call | solution.py:234
  48.4 2.0 %copy.9 = bf16[1,256,2,384]{3,2,1,0:T(2,128)(2,1)} copy(bf16[1,256,2,384]{3,2,1,0:T(2,128)(2,1)} %bitcast.7) | data formatting | bytes 786432

commit v6 on v5

--- a/solution.py
+++ b/solution.py
@@ -189,12 +189,12 @@
                 for cp in weights[l][1:]:
                     cp.wait()
             for step in steps:
+                flush(len(pending))
                 pieces = [CHUNKS[c] for c in step]
                 total = sum(4 * n for _, n in pieces)
                 mixed = jnp.concatenate([o_s[j, 2 * start:2 * (start + n), :] for start, n in pieces for j in range(2)], axis=0)
                 h = (jnp.concatenate([load_rows(c) for c in step], axis=0) + dot(mixed, wout[l])).astype(BF).astype(F32)
                 normed = layer_norm(h, gains[2:3], gains[3:4])
-                flush(len(pending))
                 for m in range(0, HID, UP):
                     hid_s[0:total, m:m + UP] = gelu(dot(normed, wup[l, :, m:m + UP])).astype(BF)
                 z = h + dot(hid_s[0:total], wdown[l])

time: 50.6 us -> 50.7 us (level)
  no operation moved by 1% of the time
where the time goes in v6:
time: 50.7 us; the launch traced here: 50.5 us
  Pallas kernels  48.5 us (96%)
  local copies, waits for them, and re-layouts  2.01 us (4%)
    pallas_call x1, Pallas kernels, local_stack(): pl.pallas_call(stack_kernel, out_shape=jax.ShapeDtypeStruct((DEV, 2, 2, D...  48.5 us
    unnamed x1, local copies, waits for them, and re-layouts  2.01 us

profile of v6, /device:TPU:1, one launch (start us, length us, event | category | flops | bytes accessed | tf_op | source)
XLA Modules:
  0.0 50.5 jit_solution(1812210994858515326)
XLA Ops:
  0.0 48.5 %stack.1 = bf16[128,2,2,384]{3,2,1,0:T(2,128)(2,1)} custom-call(bf16[2,256,384]{2,1,0:T(8,128)(2,1)} %bitcast.9, s32[256,5]{1,0:T(8,128)} %constant.2.clone.tab_ref, f32[4,4,384]{2,1,0:T(4,128)} %norms_ref.1, bf16[4,1152,384]{2,1,0:T(8,128)(2,1)} %bitcast.6, bf16[4,384,384]{2,1,0:T(8,128)(2,1)} %bitcast.8, bf16[4,384,1536]{2,1,0:T(8,128)(2,1)} %wup_ref.1, ...), custom_call_target="tpu_custom_call" | custom-call | tf_op jit(solution)/shard_map/stack/pallas_call | solution.py:234
  48.5 2.0 %copy.9 = bf16[1,256,2,384]{3,2,1,0:T(2,128)(2,1)} copy(bf16[1,256,2,384]{3,2,1,0:T(2,128)(2,1)} %bitcast.7) | data formatting | bytes 786432
